TPU v7x, 32 devices: a whole 2x2x4 slice. The times are simulated.
32 devices in a mesh: row: 4 (over y, core), col: 4 (over z), depth: 2 (over x).
Axes of the slice: x: 2, y: 2, z: 4, core: 2. Of those that a mesh axis runs over, the one named last changes fastest.
Arguments:
- diag_block: float32 [512, 512], P(('row', 'col', 'depth')), as said below
- panel_rows: float32 [32256, 512], P(('row', 'col', 'depth')), may hold values from -2 to 2
- trailing: float32 [32256, 1024], P(('row', 'depth'), 'col'), may hold values from -6 to 6
Outputs:
- diag_factor: float32 [512, 512], P(('row', 'col', 'depth'))
- panel_factor: float32 [32256, 512], P(('row', 'col', 'depth'))
- updated: float32 [32256, 1024], P(('row', 'depth'), 'col')
Inputs may be any that keep to these rules, and one draw needn't show every extreme that they name: `diag_block`: symmetric positive definite.
All inputs are finite; a program needn't handle non-finite values.
Results may differ from a plain program's by a relative error of at most 0.000062.
Values sent between devices are 32-bit elements; how exact they have to be, the bound alone decides.
A program may use at most 64 MiB of HBM per device.

v0:
```python
import functools
import math

import jax
import jax.numpy as jnp
from jax import lax
from jax.experimental import pallas as pl
from jax.experimental.pallas import tpu as pltpu
from jax.sharding import PartitionSpec as P

highest = lax.Precision.HIGHEST
AXES = ("row", "col", "depth")
LANES = 128


def dot(left, right, left_dim, right_dim):
    return lax.dot_general(
        left, right, (((left_dim,), (right_dim,)), ((), ())), precision=highest, preferred_element_type=jnp.float32
    )


def factor_block(block, halfway=None):
    size = block.shape[0]
    lane = lax.broadcasted_iota(jnp.int32, (8, size), 1)
    sub = lax.broadcasted_iota(jnp.int32, (8, size), 0)
    tiles = [block[8 * i : 8 * i + 8, :] for i in range(size // 8)]
    for j in range(size):
        if halfway is not None and j == size // 2:
            halfway()
        t, s = divmod(j, 8)
        row = tiles[t][s : s + 1, :]
        inverse = 1.0 / row[:, j : j + 1]
        source = jnp.where(lane[0:1] == j, 1.0, row) * inverse
        for i in range(t, size // 8):
            if i == t and s == 7:
                continue
            tile = tiles[i]
            new = jnp.where(lane == j, 0.0, tile) - tile[:, j : j + 1] * source
            tiles[i] = jnp.where(sub > s, new, tile) if i == t else new
    whole = jnp.concatenate(tiles, axis=0)
    r_id = lax.broadcasted_iota(jnp.int32, (size, size), 0)
    c_id = lax.broadcasted_iota(jnp.int32, (size, size), 1)
    pivots = jnp.sum(jnp.where(r_id == c_id, whole, 0.0), axis=1, keepdims=True)
    root = jnp.sqrt(pivots)
    scaled = jnp.where(r_id == c_id, 1.0, whole) / root
    inverse = jnp.where(r_id >= c_id, scaled, 0.0)
    upper = jnp.where(r_id < c_id, scaled, jnp.where(r_id == c_id, root, 0.0))
    return upper.T, inverse


def factor_all(work, low, inv, between=None):
    n = work.shape[0]
    low[...] = jnp.zeros((n, n), jnp.float32)
    inv[...] = jnp.zeros((n, n), jnp.float32)

    def step(k, carry):
        at = pl.ds(pl.multiple_of(k * LANES, LANES), LANES)
        halfway = None if between is None else functools.partial(between, k, 0)
        block_low, block_inv = factor_block(work[at, at], halfway)
        rows = lax.broadcasted_iota(jnp.int32, (n, LANES), 0)
        panel = jnp.where(rows >= (k + 1) * LANES, dot(work[:, at], block_inv, 1, 1), 0.0)
        work[...] = work[...] - dot(panel, panel, 1, 1)
        left = dot(low[at, :], inv[...], 1, 0)
        low[:, at] = panel
        low[at, at] = block_low
        inv[at, :] = -dot(block_inv, left, 1, 0)
        inv[at, at] = block_inv
        if between is not None:
            between(k, 1)
        return carry

    lax.fori_loop(0, n // LANES, step, 0)


def exchange(sizes, cuts, win_units, diag_ref, panel, low, weight, solved, held, window, pieces, work, inv, sems):
    n_r, n_c, n_d = sizes
    total = n_r * n_c * n_d
    half = n_c // 2
    units = panel.shape[0]
    (diag_s, diag_r, ring_s, ring_r, deep_s, deep_r, w1_s, w1_r, w2_s, w2_r, w3_s, w3_r, own_s) = sems
    r, c, d = lax.axis_index("row"), lax.axis_index("col"), lax.axis_index("depth")
    position = (r * n_c + c) * n_d + d

    def remote(src, dst, send, recv, **where):
        return pltpu.make_async_remote_copy(
            src_ref=src,
            dst_ref=dst,
            send_sem=send,
            recv_sem=recv,
            device_id={"row": where.get("row", r), "col": where.get("col", c), "depth": where.get("depth", d)},
            device_id_type=pl.DeviceIdType.MESH,
        )

    def taker(block):
        return lax.div(block * n_d + d, n_c)

    def slot(block):
        return jnp.where(taker(block) == d, block * n_d + d - n_c * d, n_c + block)

    def at(h):
        return pl.ds(cuts[h], cuts[h + 1] - cuts[h])

    def send_diag(k, carry):
        to = lax.rem(position + k, total)
        remote(
            diag_ref, pieces.at[position], diag_s, diag_r,
            row=lax.div(to, n_c * n_d), col=lax.rem(lax.div(to, n_d), n_c), depth=lax.rem(to, n_d),
        ).start()
        return carry

    lax.fori_loop(1, total, send_diag, 0)
    pieces[position] = diag_ref[...]

    def window_parts():
        for p in range(-(-n_c * win_units // units)):
            for b in range(n_c):
                lo, hi = max(b * win_units, p * units), min((b + 1) * win_units, (p + 1) * units)
                if lo < hi:
                    yield p, b, lo, hi - lo

    def part(p, b, lo, count):
        src = panel.at[pl.ds(lo - p * units, count)]
        dst = window.at[pl.ds(lo - b * win_units, count)]
        if p == b * n_d:
            return pltpu.make_async_copy(src, dst, w1_r.at[p])
        return remote(src, dst, w1_s.at[p, b], w1_r.at[p], row=0, col=b, depth=0)

    root = jnp.logical_and(r == 0, d == 0)
    for p, b, lo, count in window_parts():
        @pl.when(position == p)
        def _(p=p, b=b, lo=lo, count=count):
            part(p, b, lo, count).start()

    def to_depth(k):
        return remote(window, window, w2_s.at[k], w2_r, depth=k)

    def to_row(k):
        return remote(window, window, w3_s.at[k], w3_r, row=k)

    def window_second():
        for p, b, lo, count in window_parts():
            @pl.when(jnp.logical_and(root, c == b))
            def _(p=p, b=b, lo=lo, count=count):
                if p == b * n_d:
                    part(p, b, lo, count).wait()
                else:
                    piece = window.at[pl.ds(lo - b * win_units, count)]
                    pltpu.make_async_copy(piece, piece, w1_r.at[p]).wait()

        @pl.when(root)
        def _():
            for k in range(1, n_d):
                to_depth(k).start()

    def window_third():
        @pl.when(jnp.logical_and(r == 0, d != 0))
        def _():
            pltpu.make_async_copy(window, window, w2_r).wait()

        @pl.when(r == 0)
        def _():
            for k in range(1, n_r):
                to_row(k).start()

    def ring(way, s, h):
        block = lax.rem(c + n_c - s + 1, n_c) if way == 0 else lax.rem(c + s - 1, n_c)
        to = lax.rem(c + 1, n_c) if way == 0 else lax.rem(c + n_c - 1, n_c)
        dst = held.at[slot(block), at(h)]
        src = panel.at[at(h)] if s == 1 else dst
        return remote(src, dst, ring_s.at[way, s - 1, h], ring_r.at[way, s - 1, h], col=to)

    def ring_parts(s):
        return [(0, 0), (1, 1)] + ([(0, 1), (1, 0)] if s < half else [])

    def deep(step, h):
        block = lax.rem(c + n_c - step, n_c)
        to = taker(block)
        index = block * n_d + d - n_c * to
        src = panel.at[at(h)] if step == 0 else held.at[slot(block), at(h)]
        where = step + half - 1
        return to, remote(
            src, held.at[index, at(h)], deep_s.at[where, h], deep_r.at[index, h], depth=to
        )

    def start_deep(step, h):
        to, copy = deep(step, h)

        @pl.when(to != d)
        def _():
            copy.start()

    def own_copy():
        return pltpu.make_async_copy(panel, held.at[slot(c)], own_s)

    for way, h in ring_parts(1):
        ring(way, 1, h).start()
    for h in range(2):
        start_deep(0, h)

    @pl.when(taker(c) == d)
    def _():
        own_copy().start()

    def arrived(s, parts):
        for way, h in parts:
            ring(way, s, h).wait_recv()
            if s < half and (s + 1 < half or way == h):
                ring(way, s + 1, h).start()
            step = s if (way == 0 or s == half) else -s
            start_deep(step, h)

    def between(k, later):
        def when(point, action):
            if point % 2 == later:
                pl.when(k == point // 2)(action)

        when(1, window_second)
        when(3, window_third)
        if half > 1:
            when(2, lambda: arrived(1, ring_parts(1)[:2]))
            when(6, lambda: arrived(1, ring_parts(1)[2:]))

    every = pieces.at[pl.ds(0, total - 1)]
    pltpu.make_async_copy(every, every, diag_r).wait()
    mine = diag_ref.shape[0]
    for p in range(total):
        work[p * mine : (p + 1) * mine, :] = pieces[p]
    factor_all(work, low, inv, between)

    @pl.when(r != 0)
    def _():
        pltpu.make_async_copy(window, window, w3_r).wait()

    weight[...] = dot(dot(window[...].reshape(weight.shape), inv[...], 1, 1), inv[...], 1, 0)
    solved[...] = dot(panel[...].reshape(solved.shape), inv[...], 1, 1)
    for s in range(2 if half > 1 else 1, half + 1):
        arrived(s, ring_parts(s))

    for j in range(n_c):
        q = n_c * d + j

        @pl.when(lax.rem(q, n_d) != d)
        def _(j=j):
            for h in range(2):
                landed = held.at[j, at(h)]
                pltpu.make_async_copy(landed, landed, deep_r.at[j, h]).wait()

    pltpu.make_async_copy(every, every, diag_s).wait()
    for s in range(1, half + 1):
        for way, h in ring_parts(s):
            ring(way, s, h).wait_send()
    for step in range(1 - half, half + 1):
        for h in range(2):
            to, copy = deep(step, h)

            @pl.when(to != d)
            def _(copy=copy):
                copy.wait_send()

    @pl.when(taker(c) == d)
    def _():
        own_copy().wait()

    for p, b, lo, count in window_parts():
        if p != b * n_d:
            @pl.when(position == p)
            def _(p=p, b=b, lo=lo, count=count):
                part(p, b, lo, count).wait_send()

    @pl.when(root)
    def _():
        for k in range(1, n_d):
            to_depth(k).wait_send()

    @pl.when(r == 0)
    def _():
        for k in range(1, n_r):
            to_row(k).wait_send()


def exchange_call(sizes, diag_block, panel, win_units):
    n_r, n_c, n_d = sizes
    total = n_r * n_c * n_d
    units, unit, width = panel.shape
    n = diag_block.shape[1]
    square = jax.ShapeDtypeStruct((n, n), jnp.float32)
    vmem, anywhere = pl.BlockSpec(memory_space=pltpu.VMEM), pl.BlockSpec(memory_space=pl.ANY)
    dma, owners = pltpu.SemaphoreType.DMA, -(-n_c * win_units // units)
    sems = [
        dma, dma, dma((2, n_c // 2, 2)), dma((2, n_c // 2, 2)), dma((n_c, 2)), dma((n_c, 2)),
        dma((owners, n_c)), dma((owners,)), dma((n_d,)), dma, dma((n_r,)), dma, dma,
    ]
    return pl.pallas_call(
        functools.partial(exchange, sizes, (0, units // 2, units), win_units),
        out_shape=(
            square,
            jax.ShapeDtypeStruct((win_units * unit, width), jnp.float32),
            jax.ShapeDtypeStruct((units * unit, width), jnp.float32),
            jax.ShapeDtypeStruct((2 * n_c, units, unit, width), jnp.float32),
        ),
        in_specs=[vmem, vmem],
        out_specs=(vmem, vmem, vmem, anywhere),
        scratch_shapes=[
            pltpu.VMEM((win_units, unit, width), jnp.float32),
            pltpu.VMEM((total, diag_block.shape[0], n), jnp.float32),
            pltpu.VMEM((n, n), jnp.float32),
            pltpu.VMEM((n, n), jnp.float32),
            sems,
        ],
        compiler_params=pltpu.CompilerParams(has_side_effects=True),
    )(diag_block, panel)


def update(held, weight, trailing, out):
    out[...] = trailing[...] - dot(held[...], weight[...], 1, 1)


def update_call(held, weight, trailing):
    rows, columns = trailing.shape
    width = held.shape[1]
    chunk = max(m for m in range(8, 1025, 8) if rows % m == 0)
    return pl.pallas_call(
        update,
        grid=(rows // chunk,),
        out_shape=jax.ShapeDtypeStruct(trailing.shape, jnp.float32),
        in_specs=[
            pl.BlockSpec((chunk, width), lambda i: (i, 0)),
            pl.BlockSpec((columns, width), lambda i: (0, 0)),
            pl.BlockSpec((chunk, columns), lambda i: (i, 0)),
        ],
        out_specs=pl.BlockSpec((chunk, columns), lambda i: (i, 0)),
    )(held, weight, trailing)


def body(sizes, diag_block, panel_rows, trailing):
    n_r, n_c, n_d = sizes
    position = (lax.axis_index("row") * n_c + lax.axis_index("col")) * n_d + lax.axis_index("depth")
    mine = diag_block.shape[0]
    own_rows, win_rows = trailing.shape
    rows, width = panel_rows.shape
    unit = math.gcd(rows, win_rows)
    low, weight, solved, held = exchange_call(
        sizes, diag_block, panel_rows.reshape(rows // unit, unit, width), win_rows // unit
    )
    own_factor = lax.dynamic_slice_in_dim(low, position * mine, mine, 0)
    updated = update_call(held.reshape(2 * n_c * rows, width), weight, trailing)
    return (own_factor, solved, updated)


def solution(mesh):
    sizes = tuple(mesh.shape[axis] for axis in AXES)
    specs = (P(AXES, None), P(AXES, None), P(("row", "depth"), "col"))
    return jax.shard_map(
        functools.partial(body, sizes), mesh=mesh, in_specs=specs, out_specs=specs, check_vma=False
    )
```

profile of v0, /device:TPU:11, one launch (start us, length us, event | category | flops | bytes accessed | tf_op | source)
XLA Modules:
  0.0 226.0 jit_solution(11803670909469692245)
XLA Ops:
  0.6 210.9 %shard_map.58 = (f32[512,512]{1,0:T(8,128)}, f32[256,512]{1,0:T(8,128)}, f32[1008,512]{1,0:T(8,128)}, f32[8,63,16,512]{3,2,1,0:T(8,128)}) custom-call(f32[16,512]{1,0:T(8,128)} %diag_ref.1, f32[63,16,512]{2,1,0:T(8,128)} %bitcast.3), custom_call_target="tpu_custom_call" | custom-call | tf_op jit(solution)/shard_map/pallas_call | solution.py:293
  211.6 1.4 constant_dynamic-slice_fusion
  213.0 0.0 copy-start
  213.0 11.7 %shard_map.59 = f32[4032,256]{1,0:T(8,128)} custom-call(f32[8064,512]{1,0:T(8,128)} %bitcast.2, f32[256,512]{1,0:T(8,128)} %get-tuple-element.10.weight, f32[4032,256]{1,0:T(8,128)} %trailing.1), custom_call_target="tpu_custom_call" | custom-call | tf_op jit(solution)/shard_map/pallas_call | solution.py:322
  224.7 0.0 copy-done
  224.7 1.3 copy.7
Async XLA Ops:
  213.0 11.7 %copy-start = (f32[1008,512]{1,0:T(8,128)S(1)}, f32[1008,512]{1,0:T(8,128)}, u32[]{:S(2)}) copy-start(f32[1008,512]{1,0:T(8,128)} %get-tuple-element.15) | copy-start | bytes 6193156
where the time goes:
time: 229 us; the launch traced here: 226 us
  Pallas kernels  223 us (97%)
  local copies, waits for them, and re-layouts  2.69 us (1%)
    pallas_call x1, Pallas kernels, exchange_call(): pl.pallas_call(functools.partial(exchange, sizes, (0, units // 2, units),...  211 us
    pallas_call x1, Pallas kernels, update_call(): pl.pallas_call(update, grid=(rows // chunk,), out_shape=jax.ShapeDtypeStr...  11.7 us

commit v1 on v0

--- a/solution.py
+++ b/solution.py
@@ -332,8 +332,367 @@
     )(held, weight, trailing)
 
 
+def near(sizes, parts, split, diag_ref, panel, trailing, own, solved_out, updated, raw, wraw, mult, trail, solved, sent,
+         landed, pieces, work, low, inv, dense, sems):
+    n_r, n_c, n_d = sizes
+    total = n_r * n_c * n_d
+    planes = n_r // 2 * n_d
+    last = n_c - 1
+    per = n_c // n_d
+    rows = raw.shape[1]
+    size = rows // split
+    (own_s, trail_s, piece_s, dz_s, dz_r, dp_s, dp_r, dc_s, dc_r, raw_s, raw_r, w1_s, w1_r, w2_s, w2_r, w3_s, w3_r, w4_s, w4_r,
+     prod_s, prod_r, out_s, solved_s) = sems
+    r, c, d = lax.axis_index("row"), lax.axis_index("col"), lax.axis_index("depth")
+    y, core = lax.div(r, 2), lax.rem(r, 2)
+    plane = y * n_d + d
+    position = (r * n_c + c) * n_d + d
+
+    def remote(src, dst, send, recv, **where):
+        return pltpu.make_async_remote_copy(
+            src_ref=src,
+            dst_ref=dst,
+            send_sem=send,
+            recv_sem=recv,
+            device_id={"row": where.get("row", r), "col": where.get("col", c), "depth": where.get("depth", d)},
+            device_id_type=pl.DeviceIdType.MESH,
+        )
+
+    def at(h):
+        return pl.ds(pl.multiple_of(h * size, 8), size)
+
+    def landing(ref, sem):
+        pltpu.make_async_copy(ref, ref, sem).wait()
+
+    def diag_z(k):
+        return remote(diag_ref, pieces.at[core, plane, c], dz_s.at[k], dz_r, col=lax.rem(c + k, n_c))
+
+    def diag_plane(k):
+        to = lax.rem(plane + k, planes)
+        mine = pieces.at[core, plane]
+        return remote(mine, mine, dp_s.at[k], dp_r, row=lax.div(to, n_d) * 2 + core, depth=lax.rem(to, n_d))
+
+    def diag_core():
+        return remote(pieces.at[core], pieces.at[core], dc_s, dc_r, row=y * 2 + 1 - core)
+
+    takes = lax.div(c, per)
+    goes = (c < last, c > 0, takes != d)
+    comes = (c > 0, c < last, takes == d)
+    steps = ({"col": c + 1}, {"col": c - 1}, {"depth": 1 - d})
+
+    def raw_copy(way, h):
+        return remote(raw.at[0, at(h)], raw.at[way + 1, at(h)], raw_s.at[way, h], raw_r.at[way, h], **steps[way])
+
+    def raw_start(ways, hs):
+        for h in hs:
+            for way in ways:
+                pl.when(goes[way])(lambda way=way, h=h: raw_copy(way, h).start())
+
+    def first_targets(b):
+        return [b] + ([q for q in range(planes) if q != b] if b == 0 else [])
+
+    def first(i, q):
+        p, b, lo, skip, count = parts[i]
+        src, dst = raw.at[0, pl.ds(lo, count)], wraw.at[b, pl.ds(skip, count)]
+        if p == (q // n_d * 2 * n_c) * n_d + q % n_d:
+            return pltpu.make_async_copy(src, dst, w1_r.at[i])
+        return remote(src, dst, w1_s.at[i, q], w1_r.at[i], row=q // n_d * 2, col=0, depth=q % n_d)
+
+    def first_start():
+        for late in (False, True):
+            for i, (p, b, lo, skip, count) in enumerate(parts):
+                for q in first_targets(b):
+                    if (q != b) == late:
+                        pl.when(position == p)(lambda i=i, q=q: first(i, q).start())
+
+    def first_wait(q):
+        for i, (p, b, lo, skip, count) in enumerate(parts):
+            if q in first_targets(b):
+                @pl.when(jnp.logical_and(jnp.logical_and(c == 0, core == 0), plane == q))
+                def _(i=i, b=b, skip=skip, count=count):
+                    landing(wraw.at[b, pl.ds(skip, count)], w1_r.at[i])
+
+    lead = core == 0
+
+    def second(col):
+        return remote(wraw.at[plane], wraw.at[plane], w2_s.at[col], w2_r, col=col)
+
+    def second_all(act):
+        for col in range(1, n_c):
+            who = jnp.logical_and(lead, c == 0)
+            if col == last:
+                who = jnp.logical_and(who, plane == last)
+            pl.when(who)(lambda col=col: act(second(col)))
+
+    middle = jnp.logical_and(c > 0, c < last)
+    spreads = jnp.logical_and(lead, jnp.logical_or(middle, jnp.logical_and(c == last, plane == last)))
+
+    def third(k):
+        to = lax.rem(plane + k, planes)
+        return remote(
+            wraw.at[plane], wraw.at[plane], w3_s.at[k], w3_r.at[plane], row=lax.div(to, n_d) * 2, depth=lax.rem(to, n_d)
+        )
+
+    def third_start():
+        @pl.when(spreads)
+        def _():
+            landing(wraw.at[plane], w2_r)
+            for k in range(1, planes):
+                third(k).start()
+
+    def fourth(whole):
+        ref = wraw if whole else wraw.at[c]
+        return remote(ref, ref, w4_s, w4_r, row=r + 1)
+
+    def fourth_start():
+        for q in range(n_c):
+            other = plane != q
+            need = middle if q != last else jnp.logical_or(middle, c == last)
+            pl.when(jnp.logical_and(jnp.logical_and(lead, other), need))(lambda q=q: landing(wraw.at[q], w3_r.at[q]))
+        pl.when(jnp.logical_and(lead, middle))(lambda: fourth(True).start())
+        pl.when(jnp.logical_and(lead, jnp.logical_not(middle)))(lambda: fourth(False).start())
+
+    def fourth_wait():
+        pl.when(jnp.logical_and(core == 1, middle))(lambda: landing(wraw, w4_r))
+        pl.when(jnp.logical_and(core == 1, jnp.logical_not(middle)))(lambda: landing(wraw.at[c], w4_r))
+
+    load = pltpu.make_async_copy(panel, raw.at[0], own_s)
+    load.start()
+    keep = pltpu.make_async_copy(diag_ref, pieces.at[core, plane, c], piece_s)
+    keep.start()
+    fetch = pltpu.make_async_copy(trailing, trail, trail_s)
+    fetch.start()
+    for k in range(1, n_c):
+        diag_z(k).start()
+    load.wait()
+    first_start()
+    raw_start((0, 1), range(1))
+    pl.when(c > 0)(lambda: raw_start((0, 1), range(1, split)))
+    keep.wait()
+    landing(pieces.at[core, plane, pl.ds(0, n_c - 1)], dz_r)
+    for k in range(1, planes):
+        diag_plane(k).start()
+    raw_start((2,), range(split))
+    landing(pieces.at[core, pl.ds(0, planes - 1)], dp_r)
+    diag_core().start()
+    landing(pieces.at[1 - core], dc_r)
+    for p in range(total):
+        p_r, p_c, p_d = p // (n_c * n_d), p // n_d % n_c, p % n_d
+        mine = diag_ref.shape[0]
+        work[p * mine : (p + 1) * mine, :] = pieces[p_r % 2, p_r // 2 * n_d + p_d, p_c]
+
+    def second_start():
+        for q in range(planes):
+            first_wait(q)
+        second_all(lambda copy: copy.start())
+        pl.when(c == 0)(lambda: raw_start((0, 1), range(1, split)))
+
+    stages = {1: second_start, 5: third_start, 7: fourth_start}
+
+    def between(k, later):
+        for point, action in stages.items():
+            if point % 2 == later:
+                pl.when(k == point // 2)(action)
+
+    factor_all(work, low, inv, between)
+    fourth_wait()
+
+    dense[...] = dot(inv[...], inv[...], 0, 0)
+
+    def make(q, carry):
+        @pl.when(jnp.logical_or(middle, c == q))
+        def _():
+            mult[q] = dot(wraw[q], dense[...], 1, 0)
+
+        return carry
+
+    lax.fori_loop(0, n_c, make, 0)
+    for h in range(split):
+        for way in range(3):
+            pl.when(comes[way])(lambda way=way, h=h: raw_copy(way, h).wait_recv())
+
+    flip = c > last - c
+    v_c = jnp.where(flip, last - c, c)
+    v_d = jnp.where(flip, 1 - d, d)
+
+    def task(k):
+        edge = v_c == 0
+        slot = jnp.where(edge, 2, jnp.where(k == 1, 2, jnp.where(k == 3, 2 - v_d, 1)))
+        col = jnp.where(edge, 0, jnp.where(k == 0, 3, jnp.where(k == 1, 0, jnp.where(k == 2, 2, 1))))
+        deep = jnp.where(edge, 0, jnp.where(k == 1, 1, jnp.where(k == 3, 1 - v_d, 0)))
+        j = jnp.where(edge, 3, v_d)
+        active = jnp.logical_or(v_c == 1, jnp.logical_and(v_d == 1, k == 0))
+        return (
+            active,
+            jnp.where(flip, 3 - slot, slot),
+            jnp.where(flip, last - col, col),
+            jnp.where(flip, 1 - deep, deep),
+            jnp.where(flip, 3 - j, j),
+        )
+
+    def prod_copy(t):
+        k, h = lax.rem(t, 4), lax.div(t, 4)
+        active, slot, col, deep, j = task(k)
+        return active, remote(sent.at[k, at(h)], landed.at[j, at(h)], prod_s.at[k, h], prod_r.at[j, h], col=col, depth=deep)
+
+    def launch(t):
+        active, copy = prod_copy(t)
+        pl.when(active)(lambda: copy.start())
+
+    def produce(t, carry):
+        k, h = lax.rem(t, 4), lax.div(t, 4)
+        active, slot, col, deep, j = task(k)
+
+        @pl.when(active)
+        def _():
+            sent[k, at(h), :] = dot(raw[slot, at(h), :], mult[col], 1, 1)
+
+        pl.when(t > 0)(lambda: launch(t - 1))
+        return carry
+
+    lax.fori_loop(0, 4 * split, produce, 0)
+
+    def local(j):
+        cj, dj = d * per + lax.div(j, n_d), lax.rem(j, n_d)
+        same = dj == d
+        slot = jnp.where(cj == c, jnp.where(same, 0, 3), jnp.where(cj < c, 1, 2))
+        close = jnp.logical_and(cj - c < 2, c - cj < 2)
+        return jnp.logical_or(cj == c, jnp.logical_and(same, close)), slot
+
+    def spot(t):
+        return pl.ds(pl.multiple_of(t * size, 8), size)
+
+    def out_copy(t):
+        return pltpu.make_async_copy(trail.at[spot(t)], updated.at[spot(t)], out_s.at[t])
+
+    def own_rows(h, carry):
+        solved[at(h), :] = dot(raw[0, at(h), :], inv[...], 1, 1)
+        return carry
+
+    lax.fori_loop(0, split, own_rows, 0)
+    launch(4 * split - 1)
+    store = pltpu.make_async_copy(solved, solved_out, solved_s)
+    fetch.wait()
+
+    def consume(t, carry):
+        j, h = lax.div(t, split), lax.rem(t, split)
+        here, slot = local(j)
+
+        @pl.when(here)
+        def _():
+            trail[spot(t), :] = trail[spot(t), :] - dot(raw[slot, at(h), :], mult[c], 1, 1)
+
+        return carry
+
+    lax.fori_loop(0, 4 * split, consume, 0)
+    store.start()
+
+    def flush(t, carry):
+        here, slot = local(lax.div(t, split))
+        pl.when(here)(lambda: out_copy(t).start())
+        return carry
+
+    lax.fori_loop(0, 4 * split, flush, 0)
+
+    def receive(i, carry):
+        h, j = lax.div(i, 4), lax.rem(i, 4)
+        t = j * split + h
+        here, slot = local(j)
+
+        @pl.when(jnp.logical_not(here))
+        def _():
+            landing(landed.at[j, at(h)], prod_r.at[j, h])
+            trail[spot(t), :] = trail[spot(t), :] - landed[j, at(h), :]
+            out_copy(t).start()
+
+        return carry
+
+    lax.fori_loop(0, 4 * split, receive, 0)
+    mine = diag_ref.shape[0]
+    own[...] = low[pl.ds(pl.multiple_of(position * mine, 8), mine), :]
+
+    for k in range(1, n_c):
+        diag_z(k).wait_send()
+    for k in range(1, planes):
+        diag_plane(k).wait_send()
+    diag_core().wait_send()
+    for h in range(split):
+        for way in range(3):
+            pl.when(goes[way])(lambda way=way, h=h: raw_copy(way, h).wait_send())
+    for i, (p, b, lo, skip, count) in enumerate(parts):
+        for q in first_targets(b):
+            if p != (q // n_d * 2 * n_c) * n_d + q % n_d:
+                pl.when(position == p)(lambda i=i, q=q: first(i, q).wait_send())
+    second_all(lambda copy: copy.wait_send())
+
+    @pl.when(spreads)
+    def _():
+        for k in range(1, planes):
+            third(k).wait_send()
+
+    pl.when(jnp.logical_and(lead, middle))(lambda: fourth(True).wait_send())
+    pl.when(jnp.logical_and(lead, jnp.logical_not(middle)))(lambda: fourth(False).wait_send())
+
+    def drain(t, carry):
+        active, copy = prod_copy(t)
+        pl.when(active)(lambda: copy.wait_send())
+        out_copy(t).wait()
+        return carry
+
+    lax.fori_loop(0, 4 * split, drain, 0)
+    store.wait()
+
+
+def near_call(sizes, diag_block, panel, trailing):
+    n_r, n_c, n_d = sizes
+    mine, n = diag_block.shape
+    rows, width = panel.shape
+    columns = trailing.shape[1]
+    split = 2
+    planes = n_r // 2 * n_d
+    parts = []
+    for p in range(-(-n_c * columns // rows)):
+        for b in range(n_c):
+            lo, hi = max(b * columns, p * rows), min((b + 1) * columns, (p + 1) * rows)
+            if lo < hi:
+                parts.append((p, b, lo - p * rows, lo - b * columns, hi - lo))
+    vmem, anywhere = pl.BlockSpec(memory_space=pltpu.VMEM), pl.BlockSpec(memory_space=pl.ANY)
+    dma = pltpu.SemaphoreType.DMA
+    sems = [
+        dma, dma, dma, dma((n_c,)), dma, dma((planes,)), dma, dma, dma, dma((3, split)), dma((3, split)),
+        dma((len(parts), planes)), dma((len(parts),)), dma((n_c,)), dma, dma((planes,)), dma((planes,)), dma, dma,
+        dma((4, split)), dma((4, split)), dma((4 * split,)), dma,
+    ]
+    square = pltpu.VMEM((n, n), jnp.float32)
+    return pl.pallas_call(
+        functools.partial(near, sizes, parts, split),
+        out_shape=(
+            jax.ShapeDtypeStruct((mine, n), jnp.float32),
+            jax.ShapeDtypeStruct((rows, width), jnp.float32),
+            jax.ShapeDtypeStruct(trailing.shape, jnp.float32),
+        ),
+        in_specs=[vmem, anywhere, anywhere],
+        out_specs=(vmem, anywhere, anywhere),
+        scratch_shapes=[
+            pltpu.VMEM((4, rows, width), jnp.float32),
+            pltpu.VMEM((n_c, columns, width), jnp.float32),
+            pltpu.VMEM((n_c, columns, width), jnp.float32),
+            pltpu.VMEM(trailing.shape, jnp.float32),
+            pltpu.VMEM((rows, width), jnp.float32),
+            pltpu.VMEM((4, rows, columns), jnp.float32),
+            pltpu.VMEM((4, rows, columns), jnp.float32),
+            pltpu.VMEM((2, planes, n_c, mine, n), jnp.float32),
+            square, square, square, square,
+            sems,
+        ],
+        compiler_params=pltpu.CompilerParams(has_side_effects=True, vmem_limit_bytes=63000000),
+    )(diag_block, panel, trailing)
+
+
 def body(sizes, diag_block, panel_rows, trailing):
     n_r, n_c, n_d = sizes
+    if sizes == (4, 4, 2) and panel_rows.shape[0] % 16 == 0:
+        return near_call(sizes, diag_block, panel_rows, trailing)
     position = (lax.axis_index("row") * n_c + lax.axis_index("col")) * n_d + lax.axis_index("depth")
     mine = diag_block.shape[0]
     own_rows, win_rows = trailing.shape

time: 229 us -> 177 us (0.77)
  the two profiles are of different devices: /device:TPU:11 before, /device:TPU:31 now
where the time goes in v1:
time: 177 us
  Pallas kernels  170 us (96%)
  local copies, waits for them, and re-layouts  6.57 us (4%)
    pallas_call x1, Pallas kernels, near_call(): pl.pallas_call(functools.partial(near, sizes, parts, split), out_shape=(j...  170 us
    unnamed x5, local copies, waits for them, and re-layouts  6.57 us

profile of v1, /device:TPU:31, one launch (start us, length us, event | category | flops | bytes accessed | tf_op | source)
XLA Modules:
  0.0 177.2 jit_solution(8239029674919986031)
XLA Ops:
  0.6 170.0 %shard_map.58 = (f32[16,512]{1,0:T(8,128)}, f32[1008,512]{1,0:T(8,128)}, f32[4032,256]{1,0:T(8,128)}) custom-call(f32[16,512]{1,0:T(8,128)} %diag_ref.1, f32[1008,512]{1,0:T(8,128)} %panel.1, f32[4032,256]{1,0:T(8,128)} %trailing.1), custom_call_target="tpu_custom_call" | custom-call | tf_op jit(solution)/shard_map/pallas_call | solution.py:667
  170.6 0.0 copy-start
  170.6 1.5 copy.9
  172.2 3.0 %copy.10 = f32[1008,512]{1,0:T(8,128)} copy(f32[1008,512]{1,0:T(8,128)} %get-tuple-element.7) | data formatting | bytes 4128768
  175.2 0.0 copy-done
  175.2 2.0 %copy.11 = f32[4032,256]{1,0:T(8,128)} copy(f32[4032,256]{1,0:T(8,128)S(1)} %copy-done) | data formatting | bytes 8257536
Async XLA Ops:
  170.6 4.6 %copy-start = (f32[4032,256]{1,0:T(8,128)S(1)}, f32[4032,256]{1,0:T(8,128)}, u32[]{:S(2)}) copy-start(f32[4032,256]{1,0:T(8,128)} %get-tuple-element.8) | copy-start | bytes 12386308

commit v2 on v1

--- a/solution.py
+++ b/solution.py
@@ -21,22 +21,44 @@
 
 def factor_block(block, halfway=None):
     size = block.shape[0]
-    lane = lax.broadcasted_iota(jnp.int32, (8, size), 1)
-    sub = lax.broadcasted_iota(jnp.int32, (8, size), 0)
-    tiles = [block[8 * i : 8 * i + 8, :] for i in range(size // 8)]
-    for j in range(size):
-        if halfway is not None and j == size // 2:
+    step = 8
+    lane = lax.broadcasted_iota(jnp.int32, (step, size), 1)
+    sub = lax.broadcasted_iota(jnp.int32, (step, size), 0)
+    tiles = [block[step * i : step * (i + 1), :] for i in range(size // step)]
+
+    def across(tile, j):
+        return jnp.broadcast_to(tile[:, j : j + 1], (step, size))
+
+    def down(tile, s):
+        return jnp.broadcast_to(tile[s : s + 1, :], (step, size))
+
+    for t in range(size // step):
+        if halfway is not None and t == size // step // 2:
             halfway()
-        t, s = divmod(j, 8)
-        row = tiles[t][s : s + 1, :]
-        inverse = 1.0 / row[:, j : j + 1]
-        source = jnp.where(lane[0:1] == j, 1.0, row) * inverse
-        for i in range(t, size // 8):
-            if i == t and s == 7:
-                continue
-            tile = tiles[i]
-            new = jnp.where(lane == j, 0.0, tile) - tile[:, j : j + 1] * source
-            tiles[i] = jnp.where(sub > s, new, tile) if i == t else new
+        first = step * t
+        tile = tiles[t]
+        top = [across(tile, first + k) for k in range(step)]
+        source, ratio = [], []
+        for s in range(step):
+            inverse = 1.0 / down(top[s], s)
+            source.append(jnp.where(lane == first + s, 1.0, down(tile, s)) * inverse)
+            ratio.append([down(top[k], s) * inverse for k in range(s + 1, step)])
+            below = sub > s
+            for k in range(s + 1, step):
+                top[k] = jnp.where(below, top[k] - top[s] * ratio[s][k - s - 1], top[k])
+            tile = jnp.where(below, jnp.where(lane == first + s, 0.0, tile) - top[s] * source[s], tile)
+        if t + 1 < size // step:
+            total = [jnp.where((lane > first + s) & (lane < first + step), 0.0, source[s]) for s in range(step)]
+            for s in range(step - 2, -1, -1):
+                for k in range(step - 1, s, -1):
+                    total[s] = total[s] - ratio[s][k - s - 1] * total[k]
+            panel = (lane >= first) & (lane < first + step)
+            for i in range(t + 1, size // step):
+                new = jnp.where(panel, 0.0, tiles[i])
+                for s in range(step):
+                    new = new - across(tiles[i], first + s) * total[s]
+                tiles[i] = new
+        tiles[t] = tile
     whole = jnp.concatenate(tiles, axis=0)
     r_id = lax.broadcasted_iota(jnp.int32, (size, size), 0)
     c_id = lax.broadcasted_iota(jnp.int32, (size, size), 1)
@@ -341,6 +363,10 @@
     per = n_c // n_d
     rows = raw.shape[1]
     size = rows // split
+    part = wraw.shape[2]
+    cuts = (0, size // 16 * 8, size, rows)
+    raw_halves = [[(h, way) for h in range(3) for way in range(2) if (cuts[h] >= size) == bool(late)] for late in range(2)]
+    order = sorted(range(len(parts)), key=lambda i: (-parts[i][1], parts[i][2]))
     (own_s, trail_s, piece_s, dz_s, dz_r, dp_s, dp_r, dc_s, dc_r, raw_s, raw_r, w1_s, w1_r, w2_s, w2_r, w3_s, w3_r, w4_s, w4_r,
      prod_s, prod_r, out_s, solved_s) = sems
     r, c, d = lax.axis_index("row"), lax.axis_index("col"), lax.axis_index("depth")
@@ -381,80 +407,75 @@
     steps = ({"col": c + 1}, {"col": c - 1}, {"depth": 1 - d})
 
     def raw_copy(way, h):
-        return remote(raw.at[0, at(h)], raw.at[way + 1, at(h)], raw_s.at[way, h], raw_r.at[way, h], **steps[way])
+        span = pl.ds(cuts[h], cuts[h + 1] - cuts[h])
+        return remote(raw.at[0, span], raw.at[way + 1, span], raw_s.at[way, h], raw_r.at[way, h], **steps[way])
 
     def raw_start(ways, hs):
         for h in hs:
             for way in ways:
                 pl.when(goes[way])(lambda way=way, h=h: raw_copy(way, h).start())
 
-    def first_targets(b):
-        return [b] + ([q for q in range(planes) if q != b] if b == 0 else [])
-
-    def first(i, q):
-        p, b, lo, skip, count = parts[i]
-        src, dst = raw.at[0, pl.ds(lo, count)], wraw.at[b, pl.ds(skip, count)]
-        if p == (q // n_d * 2 * n_c) * n_d + q % n_d:
-            return pltpu.make_async_copy(src, dst, w1_r.at[i])
-        return remote(src, dst, w1_s.at[i, q], w1_r.at[i], row=q // n_d * 2, col=0, depth=q % n_d)
+    def first(i):
+        p, e, lo, skip, count = parts[i]
+        q, k = e // 2, e % 2
+        src, dst = raw.at[0, pl.ds(lo, count)], wraw.at[k, q, pl.ds(skip, count)]
+        row, depth = q // n_d * 2 + k, q % n_d
+        if p == row * n_c * n_d + depth:
+            return False, pltpu.make_async_copy(src, dst, w1_r.at[i])
+        return True, remote(src, dst, w1_s.at[i], w1_r.at[i], row=row, col=0, depth=depth)
 
     def first_start():
-        for late in (False, True):
-            for i, (p, b, lo, skip, count) in enumerate(parts):
-                for q in first_targets(b):
-                    if (q != b) == late:
-                        pl.when(position == p)(lambda i=i, q=q: first(i, q).start())
-
-    def first_wait(q):
-        for i, (p, b, lo, skip, count) in enumerate(parts):
-            if q in first_targets(b):
-                @pl.when(jnp.logical_and(jnp.logical_and(c == 0, core == 0), plane == q))
-                def _(i=i, b=b, skip=skip, count=count):
-                    landing(wraw.at[b, pl.ds(skip, count)], w1_r.at[i])
-
-    lead = core == 0
+        for i in order:
+            pl.when(position == parts[i][0])(lambda i=i: first(i)[1].start())
+
+    def first_wait():
+        for i, (p, e, lo, skip, count) in enumerate(parts):
+            @pl.when(jnp.logical_and(c == 0, plane * 2 + core == e))
+            def _(i=i, e=e, skip=skip, count=count):
+                landing(wraw.at[e % 2, e // 2, pl.ds(skip, count)], w1_r.at[i])
+
+    middle = jnp.logical_and(c > 0, c < last)
+    edge = jnp.logical_not(middle)
+    mine_w = wraw.at[core, plane]
 
     def second(col):
-        return remote(wraw.at[plane], wraw.at[plane], w2_s.at[col], w2_r, col=col)
+        return remote(mine_w, mine_w, w2_s.at[col], w2_r, col=col)
 
     def second_all(act):
-        for col in range(1, n_c):
-            who = jnp.logical_and(lead, c == 0)
-            if col == last:
-                who = jnp.logical_and(who, plane == last)
+        for col in [*range(last - 1, 0, -1), last]:
+            who = c == 0 if col < last else jnp.logical_and(c == 0, plane == last)
             pl.when(who)(lambda col=col: act(second(col)))
 
-    middle = jnp.logical_and(c > 0, c < last)
-    spreads = jnp.logical_and(lead, jnp.logical_or(middle, jnp.logical_and(c == last, plane == last)))
+    spreads = jnp.logical_or(middle, jnp.logical_and(plane == c, edge))
 
     def third(k):
         to = lax.rem(plane + k, planes)
-        return remote(
-            wraw.at[plane], wraw.at[plane], w3_s.at[k], w3_r.at[plane], row=lax.div(to, n_d) * 2, depth=lax.rem(to, n_d)
-        )
+        return remote(mine_w, mine_w, w3_s.at[k], w3_r.at[plane], row=lax.div(to, n_d) * 2 + core, depth=lax.rem(to, n_d))
 
     def third_start():
+        pl.when(jnp.logical_and(spreads, c > 0))(lambda: landing(mine_w, w2_r))
+
         @pl.when(spreads)
         def _():
-            landing(wraw.at[plane], w2_r)
             for k in range(1, planes):
                 third(k).start()
 
+        raw_start((2,), range(1, len(cuts) - 1))
+
     def fourth(whole):
-        ref = wraw if whole else wraw.at[c]
-        return remote(ref, ref, w4_s, w4_r, row=r + 1)
+        ref = wraw.at[core] if whole else wraw.at[core, c]
+        return remote(ref, ref, w4_s, w4_r, row=y * 2 + 1 - core)
 
     def fourth_start():
         for q in range(n_c):
-            other = plane != q
-            need = middle if q != last else jnp.logical_or(middle, c == last)
-            pl.when(jnp.logical_and(jnp.logical_and(lead, other), need))(lambda q=q: landing(wraw.at[q], w3_r.at[q]))
-        pl.when(jnp.logical_and(lead, middle))(lambda: fourth(True).start())
-        pl.when(jnp.logical_and(lead, jnp.logical_not(middle)))(lambda: fourth(False).start())
+            need = jnp.logical_and(plane != q, jnp.logical_or(middle, c == q))
+            pl.when(need)(lambda q=q: landing(wraw.at[core, q], w3_r.at[q]))
+        pl.when(middle)(lambda: fourth(True).start())
+        pl.when(edge)(lambda: fourth(False).start())
 
     def fourth_wait():
-        pl.when(jnp.logical_and(core == 1, middle))(lambda: landing(wraw, w4_r))
-        pl.when(jnp.logical_and(core == 1, jnp.logical_not(middle)))(lambda: landing(wraw.at[c], w4_r))
+        pl.when(middle)(lambda: landing(wraw.at[1 - core], w4_r))
+        pl.when(edge)(lambda: landing(wraw.at[1 - core, c], w4_r))
 
     load = pltpu.make_async_copy(panel, raw.at[0], own_s)
     load.start()
@@ -466,28 +487,25 @@
         diag_z(k).start()
     load.wait()
     first_start()
-    raw_start((0, 1), range(1))
-    pl.when(c > 0)(lambda: raw_start((0, 1), range(1, split)))
     keep.wait()
     landing(pieces.at[core, plane, pl.ds(0, n_c - 1)], dz_r)
     for k in range(1, planes):
         diag_plane(k).start()
-    raw_start((2,), range(split))
+    raw_start((0, 1), range(1))
+    pl.when(c > 0)(lambda: raw_start((0, 1), range(1, len(cuts) - 1)))
+    first_wait()
+    second_all(lambda copy: copy.start())
+    pl.when(c == 0)(lambda: raw_start((0, 1), range(1, len(cuts) - 1)))
+    raw_start((2,), range(1))
     landing(pieces.at[core, pl.ds(0, planes - 1)], dp_r)
     diag_core().start()
     landing(pieces.at[1 - core], dc_r)
+    mine = diag_ref.shape[0]
     for p in range(total):
         p_r, p_c, p_d = p // (n_c * n_d), p // n_d % n_c, p % n_d
-        mine = diag_ref.shape[0]
         work[p * mine : (p + 1) * mine, :] = pieces[p_r % 2, p_r // 2 * n_d + p_d, p_c]
 
-    def second_start():
-        for q in range(planes):
-            first_wait(q)
-        second_all(lambda copy: copy.start())
-        pl.when(c == 0)(lambda: raw_start((0, 1), range(1, split)))
-
-    stages = {1: second_start, 5: third_start, 7: fourth_start}
+    stages = {4: third_start, 7: fourth_start}
 
     def between(k, later):
         for point, action in stages.items():
@@ -497,30 +515,16 @@
     factor_all(work, low, inv, between)
     fourth_wait()
 
-    dense[...] = dot(inv[...], inv[...], 0, 0)
-
-    def make(q, carry):
-        @pl.when(jnp.logical_or(middle, c == q))
-        def _():
-            mult[q] = dot(wraw[q], dense[...], 1, 0)
-
-        return carry
-
-    lax.fori_loop(0, n_c, make, 0)
-    for h in range(split):
-        for way in range(3):
-            pl.when(comes[way])(lambda way=way, h=h: raw_copy(way, h).wait_recv())
-
     flip = c > last - c
     v_c = jnp.where(flip, last - c, c)
     v_d = jnp.where(flip, 1 - d, d)
 
     def task(k):
-        edge = v_c == 0
-        slot = jnp.where(edge, 2, jnp.where(k == 1, 2, jnp.where(k == 3, 2 - v_d, 1)))
-        col = jnp.where(edge, 0, jnp.where(k == 0, 3, jnp.where(k == 1, 0, jnp.where(k == 2, 2, 1))))
-        deep = jnp.where(edge, 0, jnp.where(k == 1, 1, jnp.where(k == 3, 1 - v_d, 0)))
-        j = jnp.where(edge, 3, v_d)
+        end = v_c == 0
+        slot = jnp.where(end, 2, jnp.where(k == 1, 2, jnp.where(k == 3, 2 - v_d, 1)))
+        col = jnp.where(end, 0, jnp.where(k == 0, 3, jnp.where(k == 1, 0, jnp.where(k == 2, 2, 1))))
+        deep = jnp.where(end, 0, jnp.where(k == 1, 1, jnp.where(k == 3, 1 - v_d, 0)))
+        j = jnp.where(end, 3, v_d)
         active = jnp.logical_or(v_c == 1, jnp.logical_and(v_d == 1, k == 0))
         return (
             active,
@@ -539,9 +543,23 @@
         active, copy = prod_copy(t)
         pl.when(active)(lambda: copy.start())
 
+    dense[...] = dot(inv[...], inv[...], 0, 0)
+    for h, way in raw_halves[0]:
+        pl.when(comes[way])(lambda way=way, h=h: raw_copy(way, h).wait_recv())
+
     def produce(t, carry):
         k, h = lax.rem(t, 4), lax.div(t, 4)
         active, slot, col, deep, j = task(k)
+
+        @pl.when(jnp.logical_and(h == 0, jnp.logical_or(middle, k == 0)))
+        def _():
+            for i in range(2):
+                mult[col, i * part : (i + 1) * part, :] = dot(wraw[i, col], dense[...], 1, 0)
+
+        @pl.when(t == 4)
+        def _():
+            for h, way in raw_halves[1]:
+                pl.when(comes[way])(lambda way=way, h=h: raw_copy(way, h).wait_recv())
 
         @pl.when(active)
         def _():
@@ -573,6 +591,8 @@
     launch(4 * split - 1)
     store = pltpu.make_async_copy(solved, solved_out, solved_s)
     fetch.wait()
+    for h in range(len(cuts) - 1):
+        pl.when(comes[2])(lambda h=h: raw_copy(2, h).wait_recv())
 
     def consume(t, carry):
         j, h = lax.div(t, split), lax.rem(t, split)
@@ -608,7 +628,6 @@
         return carry
 
     lax.fori_loop(0, 4 * split, receive, 0)
-    mine = diag_ref.shape[0]
     own[...] = low[pl.ds(pl.multiple_of(position * mine, 8), mine), :]
 
     for k in range(1, n_c):
@@ -616,13 +635,13 @@
     for k in range(1, planes):
         diag_plane(k).wait_send()
     diag_core().wait_send()
-    for h in range(split):
+    for h in range(len(cuts) - 1):
         for way in range(3):
             pl.when(goes[way])(lambda way=way, h=h: raw_copy(way, h).wait_send())
-    for i, (p, b, lo, skip, count) in enumerate(parts):
-        for q in first_targets(b):
-            if p != (q // n_d * 2 * n_c) * n_d + q % n_d:
-                pl.when(position == p)(lambda i=i, q=q: first(i, q).wait_send())
+    for i in order:
+        far, copy = first(i)
+        if far:
+            pl.when(position == parts[i][0])(lambda copy=copy: copy.wait_send())
     second_all(lambda copy: copy.wait_send())
 
     @pl.when(spreads)
@@ -630,8 +649,8 @@
         for k in range(1, planes):
             third(k).wait_send()
 
-    pl.when(jnp.logical_and(lead, middle))(lambda: fourth(True).wait_send())
-    pl.when(jnp.logical_and(lead, jnp.logical_not(middle)))(lambda: fourth(False).wait_send())
+    pl.when(middle)(lambda: fourth(True).wait_send())
+    pl.when(edge)(lambda: fourth(False).wait_send())
 
     def drain(t, carry):
         active, copy = prod_copy(t)
@@ -651,16 +670,17 @@
     split = 2
     planes = n_r // 2 * n_d
     parts = []
+    part = columns // 2
     for p in range(-(-n_c * columns // rows)):
-        for b in range(n_c):
-            lo, hi = max(b * columns, p * rows), min((b + 1) * columns, (p + 1) * rows)
+        for e in range(2 * n_c):
+            lo, hi = max(e * part, p * rows), min((e + 1) * part, (p + 1) * rows)
             if lo < hi:
-                parts.append((p, b, lo - p * rows, lo - b * columns, hi - lo))
+                parts.append((p, e, lo - p * rows, lo - e * part, hi - lo))
     vmem, anywhere = pl.BlockSpec(memory_space=pltpu.VMEM), pl.BlockSpec(memory_space=pl.ANY)
     dma = pltpu.SemaphoreType.DMA
     sems = [
-        dma, dma, dma, dma((n_c,)), dma, dma((planes,)), dma, dma, dma, dma((3, split)), dma((3, split)),
-        dma((len(parts), planes)), dma((len(parts),)), dma((n_c,)), dma, dma((planes,)), dma((planes,)), dma, dma,
+        dma, dma, dma, dma((n_c,)), dma, dma((planes,)), dma, dma, dma, dma((3, 3)), dma((3, 3)),
+        dma((len(parts),)), dma((len(parts),)), dma((n_c,)), dma, dma((planes,)), dma((planes,)), dma, dma,
         dma((4, split)), dma((4, split)), dma((4 * split,)), dma,
     ]
     square = pltpu.VMEM((n, n), jnp.float32)
@@ -675,7 +695,7 @@
         out_specs=(vmem, anywhere, anywhere),
         scratch_shapes=[
             pltpu.VMEM((4, rows, width), jnp.float32),
-            pltpu.VMEM((n_c, columns, width), jnp.float32),
+            pltpu.VMEM((2, n_c, part, width), jnp.float32),
             pltpu.VMEM((n_c, columns, width), jnp.float32),
             pltpu.VMEM(trailing.shape, jnp.float32),
             pltpu.VMEM((rows, width), jnp.float32),

time: 177 us -> 123 us (0.69)
  the two profiles are of different devices: /device:TPU:31 before, /device:TPU:11 now
where the time goes in v2:
time: 123 us; the launch traced here: 122 us
  Pallas kernels  115 us (93%)
  local copies, waits for them, and re-layouts  6.57 us (5%)
    pallas_call x1, Pallas kernels, near_call(): pl.pallas_call(functools.partial(near, sizes, parts, split), out_shape=(j...  115 us
    unnamed x5, local copies, waits for them, and re-layouts  6.57 us

profile of v2, /device:TPU:11, one launch (start us, length us, event | category | flops | bytes accessed | tf_op | source)
XLA Modules:
  0.0 121.7 jit_solution(2602896483525184821)
XLA Ops:
  0.6 114.5 %shard_map.58 = (f32[16,512]{1,0:T(8,128)}, f32[1008,512]{1,0:T(8,128)}, f32[4032,256]{1,0:T(8,128)}) custom-call(f32[16,512]{1,0:T(8,128)} %diag_ref.1, f32[1008,512]{1,0:T(8,128)} %panel.1, f32[4032,256]{1,0:T(8,128)} %trailing.1), custom_call_target="tpu_custom_call" | custom-call | tf_op jit(solution)/shard_map/pallas_call | solution.py:687
  115.1 0.0 copy-start
  115.2 1.5 %copy.9 = f32[16,512]{1,0:T(8,128)} copy(f32[16,512]{1,0:T(8,128)} %get-tuple-element.6) | data formatting | bytes 65536
  116.7 3.0 %copy.10 = f32[1008,512]{1,0:T(8,128)} copy(f32[1008,512]{1,0:T(8,128)} %get-tuple-element.7) | data formatting | bytes 4128768
  119.7 0.0 copy-done
  119.7 2.0 %copy.11 = f32[4032,256]{1,0:T(8,128)} copy(f32[4032,256]{1,0:T(8,128)S(1)} %copy-done) | data formatting | bytes 8257536
Async XLA Ops:
  115.1 4.6 %copy-start = (f32[4032,256]{1,0:T(8,128)S(1)}, f32[4032,256]{1,0:T(8,128)}, u32[]{:S(2)}) copy-start(f32[4032,256]{1,0:T(8,128)} %get-tuple-element.8) | copy-start | bytes 12386308

commit v3 on v2

--- a/solution.py
+++ b/solution.py
@@ -354,7 +354,7 @@
     )(held, weight, trailing)
 
 
-def near(sizes, parts, split, diag_ref, panel, trailing, own, solved_out, updated, raw, wraw, mult, trail, solved, sent,
+def near(sizes, parts, split, diag_ref, panel, trailing, own, solved, trail, raw, wraw, mult, sent,
          landed, pieces, work, low, inv, dense, sems):
     n_r, n_c, n_d = sizes
     total = n_r * n_c * n_d
@@ -368,7 +368,7 @@
     raw_halves = [[(h, way) for h in range(3) for way in range(2) if (cuts[h] >= size) == bool(late)] for late in range(2)]
     order = sorted(range(len(parts)), key=lambda i: (-parts[i][1], parts[i][2]))
     (own_s, trail_s, piece_s, dz_s, dz_r, dp_s, dp_r, dc_s, dc_r, raw_s, raw_r, w1_s, w1_r, w2_s, w2_r, w3_s, w3_r, w4_s, w4_r,
-     prod_s, prod_r, out_s, solved_s) = sems
+     prod_s, prod_r) = sems
     r, c, d = lax.axis_index("row"), lax.axis_index("col"), lax.axis_index("depth")
     y, core = lax.div(r, 2), lax.rem(r, 2)
     plane = y * n_d + d
@@ -391,7 +391,7 @@
         pltpu.make_async_copy(ref, ref, sem).wait()
 
     def diag_z(k):
-        return remote(diag_ref, pieces.at[core, plane, c], dz_s.at[k], dz_r, col=lax.rem(c + k, n_c))
+        return remote(pieces.at[core, plane, c], pieces.at[core, plane, c], dz_s.at[k], dz_r, col=lax.rem(c + k, n_c))
 
     def diag_plane(k):
         to = lax.rem(plane + k, planes)
@@ -477,17 +477,33 @@
         pl.when(middle)(lambda: landing(wraw.at[1 - core], w4_r))
         pl.when(edge)(lambda: landing(wraw.at[1 - core, c], w4_r))
 
+    keep = pltpu.make_async_copy(diag_ref, pieces.at[core, plane, c], piece_s)
+    keep.start()
     load = pltpu.make_async_copy(panel, raw.at[0], own_s)
     load.start()
-    keep = pltpu.make_async_copy(diag_ref, pieces.at[core, plane, c], piece_s)
-    keep.start()
     fetch = pltpu.make_async_copy(trailing, trail, trail_s)
     fetch.start()
+    gate = pltpu.get_barrier_semaphore()
+    ring = n_c * n_d
+    for k in range(1, ring):
+        to = lax.rem(c * n_d + d + k, ring)
+        pl.semaphore_signal(
+            gate, inc=1, device_id={"row": r, "col": lax.div(to, n_d), "depth": lax.rem(to, n_d)},
+            device_id_type=pl.DeviceIdType.MESH,
+        )
+    for k in range(1, n_r * n_d):
+        to = lax.rem(r * n_d + d + k, n_r * n_d)
+        far = lax.div(to, n_d) != r
+        pl.when(far)(lambda to=to: pl.semaphore_signal(
+            gate, inc=1, device_id={"row": lax.div(to, n_d), "col": c, "depth": lax.rem(to, n_d)},
+            device_id_type=pl.DeviceIdType.MESH,
+        ))
+    pl.semaphore_wait(gate, ring - 1 + (n_r - 1) * n_d)
+    keep.wait()
     for k in range(1, n_c):
         diag_z(k).start()
     load.wait()
     first_start()
-    keep.wait()
     landing(pieces.at[core, plane, pl.ds(0, n_c - 1)], dz_r)
     for k in range(1, planes):
         diag_plane(k).start()
@@ -580,16 +596,12 @@
     def spot(t):
         return pl.ds(pl.multiple_of(t * size, 8), size)
 
-    def out_copy(t):
-        return pltpu.make_async_copy(trail.at[spot(t)], updated.at[spot(t)], out_s.at[t])
-
     def own_rows(h, carry):
         solved[at(h), :] = dot(raw[0, at(h), :], inv[...], 1, 1)
         return carry
 
     lax.fori_loop(0, split, own_rows, 0)
     launch(4 * split - 1)
-    store = pltpu.make_async_copy(solved, solved_out, solved_s)
     fetch.wait()
     for h in range(len(cuts) - 1):
         pl.when(comes[2])(lambda h=h: raw_copy(2, h).wait_recv())
@@ -605,14 +617,6 @@
         return carry
 
     lax.fori_loop(0, 4 * split, consume, 0)
-    store.start()
-
-    def flush(t, carry):
-        here, slot = local(lax.div(t, split))
-        pl.when(here)(lambda: out_copy(t).start())
-        return carry
-
-    lax.fori_loop(0, 4 * split, flush, 0)
 
     def receive(i, carry):
         h, j = lax.div(i, 4), lax.rem(i, 4)
@@ -623,7 +627,6 @@
         def _():
             landing(landed.at[j, at(h)], prod_r.at[j, h])
             trail[spot(t), :] = trail[spot(t), :] - landed[j, at(h), :]
-            out_copy(t).start()
 
         return carry
 
@@ -655,11 +658,9 @@
     def drain(t, carry):
         active, copy = prod_copy(t)
         pl.when(active)(lambda: copy.wait_send())
-        out_copy(t).wait()
         return carry
 
     lax.fori_loop(0, 4 * split, drain, 0)
-    store.wait()
 
 
 def near_call(sizes, diag_block, panel, trailing):
@@ -681,7 +682,7 @@
     sems = [
         dma, dma, dma, dma((n_c,)), dma, dma((planes,)), dma, dma, dma, dma((3, 3)), dma((3, 3)),
         dma((len(parts),)), dma((len(parts),)), dma((n_c,)), dma, dma((planes,)), dma((planes,)), dma, dma,
-        dma((4, split)), dma((4, split)), dma((4 * split,)), dma,
+        dma((4, split)), dma((4, split)),
     ]
     square = pltpu.VMEM((n, n), jnp.float32)
     return pl.pallas_call(
@@ -691,22 +692,20 @@
             jax.ShapeDtypeStruct((rows, width), jnp.float32),
             jax.ShapeDtypeStruct(trailing.shape, jnp.float32),
         ),
-        in_specs=[vmem, anywhere, anywhere],
-        out_specs=(vmem, anywhere, anywhere),
+        in_specs=[pl.BlockSpec(memory_space=pltpu.HBM)] * 3,
+        out_specs=(vmem, vmem, vmem),
         scratch_shapes=[
             pltpu.VMEM((4, rows, width), jnp.float32),
             pltpu.VMEM((2, n_c, part, width), jnp.float32),
             pltpu.VMEM((n_c, columns, width), jnp.float32),
-            pltpu.VMEM(trailing.shape, jnp.float32),
-            pltpu.VMEM((rows, width), jnp.float32),
             pltpu.VMEM((4, rows, columns), jnp.float32),
             pltpu.VMEM((4, rows, columns), jnp.float32),
             pltpu.VMEM((2, planes, n_c, mine, n), jnp.float32),
             square, square, square, square,
             sems,
         ],
-        compiler_params=pltpu.CompilerParams(has_side_effects=True, vmem_limit_bytes=63000000),
-    )(diag_block, panel, trailing)
+        compiler_params=pltpu.CompilerParams(collective_id=0, has_side_effects=True, vmem_limit_bytes=40000000),
+    )(*(pltpu.with_memory_space_constraint(x, pltpu.HBM) for x in (diag_block, panel, trailing)))
 
 
 def body(sizes, diag_block, panel_rows, trailing):

time: 123 us -> 116 us (0.943)
  Pallas kernels: 115 us -> 110 us
  local copies, waits for them, and re-layouts: 6.57 us -> 3.91 us
    pallas_call x1, Pallas kernels: 115 us -> 110 us  [near_call(): pl.pallas_call(functools.partial(near, sizes, parts, split), out_shape=(j...]
    unnamed x5 -> x3, local copies, waits for them, and re-layouts: 6.57 us -> 3.91 us
where the time goes in v3:
time: 116 us; the launch traced here: 115 us
  Pallas kernels  110 us (95%)
  local copies, waits for them, and re-layouts  3.91 us (3%)
    pallas_call x1, Pallas kernels, near_call(): pl.pallas_call(functools.partial(near, sizes, parts, split), out_shape=(j...  110 us
    unnamed x3, local copies, waits for them, and re-layouts  3.91 us

profile of v3, /device:TPU:11, one launch (start us, length us, event | category | flops | bytes accessed | tf_op | source)
XLA Modules:
  0.0 114.6 jit_solution(436260582721638019)
XLA Ops:
  0.6 110.0 %shard_map.58 = (f32[16,512]{1,0:T(8,128)S(1)}, f32[1008,512]{1,0:T(8,128)S(1)}, f32[4032,256]{1,0:T(8,128)S(1)}) custom-call(f32[16,512]{1,0:T(8,128)} %diag_ref.1, f32[1008,512]{1,0:T(8,128)} %panel.1, f32[4032,256]{1,0:T(8,128)} %trailing.1), custom_call_target="tpu_custom_call" | custom-call | tf_op jit(solution)/shard_map/pallas_call | solution.py:688
  110.7 0.6 copy.9
  111.3 1.3 %copy.10 = f32[1008,512]{1,0:T(8,128)} copy(f32[1008,512]{1,0:T(8,128)S(1)} %get-tuple-element.7) | data formatting | bytes 4128768
  112.6 2.0 %copy.11 = f32[4032,256]{1,0:T(8,128)} copy(f32[4032,256]{1,0:T(8,128)S(1)} %get-tuple-element.8) | data formatting | bytes 8257536

commit v4 on v3

--- a/solution.py
+++ b/solution.py
@@ -363,10 +363,8 @@
     per = n_c // n_d
     rows = raw.shape[1]
     size = rows // split
-    part = wraw.shape[2]
     cuts = (0, size // 16 * 8, size, rows)
     raw_halves = [[(h, way) for h in range(3) for way in range(2) if (cuts[h] >= size) == bool(late)] for late in range(2)]
-    order = sorted(range(len(parts)), key=lambda i: (-parts[i][1], parts[i][2]))
     (own_s, trail_s, piece_s, dz_s, dz_r, dp_s, dp_r, dc_s, dc_r, raw_s, raw_r, w1_s, w1_r, w2_s, w2_r, w3_s, w3_r, w4_s, w4_r,
      prod_s, prod_r) = sems
     r, c, d = lax.axis_index("row"), lax.axis_index("col"), lax.axis_index("depth")
@@ -416,66 +414,89 @@
                 pl.when(goes[way])(lambda way=way, h=h: raw_copy(way, h).start())
 
     def first(i):
-        p, e, lo, skip, count = parts[i]
-        q, k = e // 2, e % 2
-        src, dst = raw.at[0, pl.ds(lo, count)], wraw.at[k, q, pl.ds(skip, count)]
-        row, depth = q // n_d * 2 + k, q % n_d
+        p, q, k, to, lo, skip, count = parts[i]
+        src, dst = raw.at[0, pl.ds(lo, count)], wraw.at[k, to, q, pl.ds(skip, count)]
+        row, depth = to // n_d * 2 + k, to % n_d
         if p == row * n_c * n_d + depth:
             return False, pltpu.make_async_copy(src, dst, w1_r.at[i])
         return True, remote(src, dst, w1_s.at[i], w1_r.at[i], row=row, col=0, depth=depth)
 
     def first_start():
-        for i in order:
-            pl.when(position == parts[i][0])(lambda i=i: first(i)[1].start())
+        for p in sorted({entry[0] for entry in parts}):
+            @pl.when(position == p)
+            def _(p=p):
+                for i in range(len(parts)):
+                    if parts[i][0] == p:
+                        first(i)[1].start()
 
     def first_wait():
-        for i, (p, e, lo, skip, count) in enumerate(parts):
-            @pl.when(jnp.logical_and(c == 0, plane * 2 + core == e))
-            def _(i=i, e=e, skip=skip, count=count):
-                landing(wraw.at[e % 2, e // 2, pl.ds(skip, count)], w1_r.at[i])
+        for to in range(planes):
+            for k in range(2):
+                @pl.when(jnp.logical_and(c == 0, jnp.logical_and(plane == to, core == k)))
+                def _(to=to, k=k):
+                    for i, (p, q, k_i, to_i, lo, skip, count) in enumerate(parts):
+                        if (k_i, to_i) == (k, to):
+                            landing(wraw.at[k, to, q, pl.ds(skip, count)], w1_r.at[i])
 
     middle = jnp.logical_and(c > 0, c < last)
     edge = jnp.logical_not(middle)
-    mine_w = wraw.at[core, plane]
 
     def second(col):
-        return remote(mine_w, mine_w, w2_s.at[col], w2_r, col=col)
+        ref = wraw.at[core, plane] if col < last else wraw.at[core, plane, last]
+        return remote(ref, ref, w2_s.at[col], w2_r, col=col)
 
     def second_all(act):
-        for col in [*range(last - 1, 0, -1), last]:
-            who = c == 0 if col < last else jnp.logical_and(c == 0, plane == last)
-            pl.when(who)(lambda col=col: act(second(col)))
-
-    spreads = jnp.logical_or(middle, jnp.logical_and(plane == c, edge))
-
-    def third(k):
+        @pl.when(c == 0)
+        def _():
+            for col in [*range(last - 1, 0, -1), last]:
+                act(second(col))
+
+    turn = [jnp.where(c > last - c, q, last - q) for q in range(n_c)]
+
+    def third(k, q):
         to = lax.rem(plane + k, planes)
-        return remote(mine_w, mine_w, w3_s.at[k], w3_r.at[plane], row=lax.div(to, n_d) * 2 + core, depth=lax.rem(to, n_d))
+        ref = wraw.at[core, plane, q]
+        return remote(
+            ref, ref, w3_s.at[k, q], w3_r.at[plane, q], row=lax.div(to, n_d) * 2 + core, depth=lax.rem(to, n_d)
+        )
+
+    def third_all(act):
+        @pl.when(middle)
+        def _():
+            for q in turn:
+                for k in range(1, planes):
+                    act(third(k, q))
+
+        @pl.when(edge)
+        def _():
+            for k in range(1, planes):
+                act(third(k, c))
 
     def third_start():
-        pl.when(jnp.logical_and(spreads, c > 0))(lambda: landing(mine_w, w2_r))
-
-        @pl.when(spreads)
-        def _():
-            for k in range(1, planes):
-                third(k).start()
-
+        pl.when(middle)(lambda: landing(wraw.at[core, plane], w2_r))
+        pl.when(c == last)(lambda: landing(wraw.at[core, plane, last], w2_r))
+        third_all(lambda copy: copy.start())
         raw_start((2,), range(1, len(cuts) - 1))
 
-    def fourth(whole):
-        ref = wraw.at[core] if whole else wraw.at[core, c]
-        return remote(ref, ref, w4_s, w4_r, row=y * 2 + 1 - core)
+    def fourth(q):
+        ref = wraw.at[core, pl.ds(0, planes), q]
+        return remote(ref, ref, w4_s.at[q], w4_r.at[q], row=y * 2 + 1 - core)
 
     def fourth_start():
-        for q in range(n_c):
-            need = jnp.logical_and(plane != q, jnp.logical_or(middle, c == q))
-            pl.when(need)(lambda q=q: landing(wraw.at[core, q], w3_r.at[q]))
-        pl.when(middle)(lambda: fourth(True).start())
-        pl.when(edge)(lambda: fourth(False).start())
-
-    def fourth_wait():
-        pl.when(middle)(lambda: landing(wraw.at[1 - core], w4_r))
-        pl.when(edge)(lambda: landing(wraw.at[1 - core, c], w4_r))
+        def pass_on(q):
+            for to in range(planes):
+                pl.when(plane != to)(lambda to=to: landing(wraw.at[core, to, q], w3_r.at[to, q]))
+            fourth(q).start()
+
+        @pl.when(middle)
+        def _():
+            for q in turn:
+                pass_on(q)
+
+        pl.when(edge)(lambda: pass_on(c))
+
+    def fourth_wait(q):
+        landing(wraw.at[1 - core, pl.ds(0, planes), q], w4_r.at[q])
 
     keep = pltpu.make_async_copy(diag_ref, pieces.at[core, plane, c], piece_s)
     keep.start()
@@ -504,11 +525,11 @@
         diag_z(k).start()
     load.wait()
     first_start()
+    raw_start((0, 1), range(1))
+    pl.when(c > 0)(lambda: raw_start((0, 1), range(1, len(cuts) - 1)))
     landing(pieces.at[core, plane, pl.ds(0, n_c - 1)], dz_r)
     for k in range(1, planes):
         diag_plane(k).start()
-    raw_start((0, 1), range(1))
-    pl.when(c > 0)(lambda: raw_start((0, 1), range(1, len(cuts) - 1)))
     first_wait()
     second_all(lambda copy: copy.start())
     pl.when(c == 0)(lambda: raw_start((0, 1), range(1, len(cuts) - 1)))
@@ -521,7 +542,7 @@
         p_r, p_c, p_d = p // (n_c * n_d), p // n_d % n_c, p % n_d
         work[p * mine : (p + 1) * mine, :] = pieces[p_r % 2, p_r // 2 * n_d + p_d, p_c]
 
-    stages = {4: third_start, 7: fourth_start}
+    stages = {2: third_start, 6: fourth_start}
 
     def between(k, later):
         for point, action in stages.items():
@@ -529,7 +550,6 @@
                 pl.when(k == point // 2)(action)
 
     factor_all(work, low, inv, between)
-    fourth_wait()
 
     flip = c > last - c
     v_c = jnp.where(flip, last - c, c)
@@ -569,8 +589,8 @@
 
         @pl.when(jnp.logical_and(h == 0, jnp.logical_or(middle, k == 0)))
         def _():
-            for i in range(2):
-                mult[col, i * part : (i + 1) * part, :] = dot(wraw[i, col], dense[...], 1, 0)
+            fourth_wait(col)
+            mult[col] = dot(wraw[:, :, col].reshape(mult.shape[1:]), dense[...], 1, 0)
 
         @pl.when(t == 4)
         def _():
@@ -641,19 +661,25 @@
     for h in range(len(cuts) - 1):
         for way in range(3):
             pl.when(goes[way])(lambda way=way, h=h: raw_copy(way, h).wait_send())
-    for i in order:
-        far, copy = first(i)
-        if far:
-            pl.when(position == parts[i][0])(lambda copy=copy: copy.wait_send())
+    for p in sorted({entry[0] for entry in parts}):
+        @pl.when(position == p)
+        def _(p=p):
+            for i in range(len(parts)):
+                if parts[i][0] == p:
+                    far, copy = first(i)
+                    if far:
+                        copy.wait_send()
+
     second_all(lambda copy: copy.wait_send())
 
-    @pl.when(spreads)
+    third_all(lambda copy: copy.wait_send())
+
+    @pl.when(middle)
     def _():
-        for k in range(1, planes):
-            third(k).wait_send()
-
-    pl.when(middle)(lambda: fourth(True).wait_send())
-    pl.when(edge)(lambda: fourth(False).wait_send())
+        for q in range(n_c):
+            fourth(q).wait_send()
+
+    pl.when(edge)(lambda: fourth(c).wait_send())
 
     def drain(t, carry):
         active, copy = prod_copy(t)
@@ -661,6 +687,29 @@
         return carry
 
     lax.fori_loop(0, 4 * split, drain, 0)
+
+
+def place(own, solved, updated, own_out, solved_out, updated_out, sems):
+    copies = [
+        pltpu.make_async_copy(src, dst, sems.at[i])
+        for i, (src, dst) in enumerate(((updated, updated_out), (solved, solved_out), (own, own_out)))
+    ]
+    for copy in copies:
+        copy.start()
+    for copy in copies:
+        copy.wait()
+
+
+def place_call(*arrays):
+    anywhere = pl.BlockSpec(memory_space=pl.ANY)
+    return pl.pallas_call(
+        place,
+        out_shape=tuple(jax.ShapeDtypeStruct(x.shape, x.dtype) for x in arrays),
+        in_specs=[anywhere] * 3,
+        out_specs=(anywhere,) * 3,
+        scratch_shapes=[pltpu.SemaphoreType.DMA((3,))],
+        compiler_params=pltpu.CompilerParams(vmem_limit_bytes=1000000),
+    )(*arrays)
 
 
 def near_call(sizes, diag_block, panel, trailing):
@@ -670,18 +719,20 @@
     columns = trailing.shape[1]
     split = 2
     planes = n_r // 2 * n_d
+    piece = columns // (2 * planes)
     parts = []
-    part = columns // 2
-    for p in range(-(-n_c * columns // rows)):
-        for e in range(2 * n_c):
-            lo, hi = max(e * part, p * rows), min((e + 1) * part, (p + 1) * rows)
-            if lo < hi:
-                parts.append((p, e, lo - p * rows, lo - e * part, hi - lo))
+    for to in range(planes - 1, -1, -1):
+        for k in range(2):
+            for q in range(n_c):
+                start = q * columns + (k * planes + to) * piece
+                for p in range(start // rows, (start + piece - 1) // rows + 1):
+                    lo, hi = max(start, p * rows), min(start + piece, (p + 1) * rows)
+                    parts.append((p, q, k, to, lo - p * rows, lo - start, hi - lo))
     vmem, anywhere = pl.BlockSpec(memory_space=pltpu.VMEM), pl.BlockSpec(memory_space=pl.ANY)
     dma = pltpu.SemaphoreType.DMA
     sems = [
         dma, dma, dma, dma((n_c,)), dma, dma((planes,)), dma, dma, dma, dma((3, 3)), dma((3, 3)),
-        dma((len(parts),)), dma((len(parts),)), dma((n_c,)), dma, dma((planes,)), dma((planes,)), dma, dma,
+        dma((len(parts),)), dma((len(parts),)), dma((n_c,)), dma, dma((planes, n_c)), dma((planes, n_c)), dma((n_c,)), dma((n_c,)),
         dma((4, split)), dma((4, split)),
     ]
     square = pltpu.VMEM((n, n), jnp.float32)
@@ -696,7 +747,7 @@
         out_specs=(vmem, vmem, vmem),
         scratch_shapes=[
             pltpu.VMEM((4, rows, width), jnp.float32),
-            pltpu.VMEM((2, n_c, part, width), jnp.float32),
+            pltpu.VMEM((2, planes, n_c, piece, width), jnp.float32),
             pltpu.VMEM((n_c, columns, width), jnp.float32),
             pltpu.VMEM((4, rows, columns), jnp.float32),
             pltpu.VMEM((4, rows, columns), jnp.float32),
@@ -711,7 +762,7 @@
 def body(sizes, diag_block, panel_rows, trailing):
     n_r, n_c, n_d = sizes
     if sizes == (4, 4, 2) and panel_rows.shape[0] % 16 == 0:
-        return near_call(sizes, diag_block, panel_rows, trailing)
+        return place_call(*near_call(sizes, diag_block, panel_rows, trailing))
     position = (lax.axis_index("row") * n_c + lax.axis_index("col")) * n_d + lax.axis_index("depth")
     mine = diag_block.shape[0]
     own_rows, win_rows = trailing.shape

time: 116 us -> 113 us (0.974); the launches traced: 115 us -> 113 us
  local copies, waits for them, and re-layouts: 3.91 us -> 0 us
  Pallas kernels: 110 us -> 112 us
    unnamed x3 -> x0, local copies, waits for them, and re-layouts: 3.91 us -> none
    pallas_call x0 -> x1, Pallas kernels: none -> 2.69 us  [place_call(): pl.pallas_call(place, out_shape=tuple((jax.ShapeDtypeStruct(x.shape, x.dt...]
where the time goes in v4:
time: 113 us
  Pallas kernels  112 us (99%)
    pallas_call x1, Pallas kernels, near_call(): pl.pallas_call(functools.partial(near, sizes, parts, split), out_shape=(j...  110 us
    pallas_call x1, Pallas kernels, place_call(): pl.pallas_call(place, out_shape=tuple((jax.ShapeDtypeStruct(x.shape, x.dt...  2.69 us

profile of v4, /device:TPU:11, one launch (start us, length us, event | category | flops | bytes accessed | tf_op | source)
XLA Modules:
  0.0 113.0 jit_solution(10006729231818504108)
XLA Ops:
  0.6 109.6 %shard_map.58 = (f32[16,512]{1,0:T(8,128)S(1)}, f32[1008,512]{1,0:T(8,128)S(1)}, f32[4032,256]{1,0:T(8,128)S(1)}) custom-call(f32[16,512]{1,0:T(8,128)} %diag_ref.1, f32[1008,512]{1,0:T(8,128)} %panel.1, f32[4032,256]{1,0:T(8,128)} %trailing.1), custom_call_target="tpu_custom_call" | custom-call | tf_op jit(solution)/shard_map/pallas_call | solution.py:739
  110.3 2.7 %shard_map.59 = (f32[16,512]{1,0:T(8,128)}, f32[1008,512]{1,0:T(8,128)}, f32[4032,256]{1,0:T(8,128)}) custom-call(f32[16,512]{1,0:T(8,128)S(1)} %get-tuple-element.6.own, f32[1008,512]{1,0:T(8,128)S(1)} %get-tuple-element.7.solved, f32[4032,256]{1,0:T(8,128)S(1)} %get-tuple-element.8.updated), custom_call_target="tpu_custom_call" | custom-call | tf_op jit(solution)/shard_map/pallas_call | solution.py:705

commit v5 on v4

--- a/solution.py
+++ b/solution.py
@@ -363,8 +363,8 @@
     per = n_c // n_d
     rows = raw.shape[1]
     size = rows // split
-    cuts = (0, size // 16 * 8, size, rows)
-    raw_halves = [[(h, way) for h in range(3) for way in range(2) if (cuts[h] >= size) == bool(late)] for late in range(2)]
+    sixth = rows // 6
+    cuts = (0, sixth, 2 * sixth, 4 * sixth, rows)
     (own_s, trail_s, piece_s, dz_s, dz_r, dp_s, dp_r, dc_s, dc_r, raw_s, raw_r, w1_s, w1_r, w2_s, w2_r, w3_s, w3_r, w4_s, w4_r,
      prod_s, prod_r) = sems
     r, c, d = lax.axis_index("row"), lax.axis_index("col"), lax.axis_index("depth")
@@ -580,8 +580,11 @@
         pl.when(active)(lambda: copy.start())
 
     dense[...] = dot(inv[...], inv[...], 0, 0)
-    for h, way in raw_halves[0]:
-        pl.when(comes[way])(lambda way=way, h=h: raw_copy(way, h).wait_recv())
+    def raw_wait(now):
+        for i in range(len(cuts) - 1):
+            if cuts[i] // size == now:
+                for way in range(2):
+                    pl.when(comes[way])(lambda way=way, i=i: raw_copy(way, i).wait_recv())
 
     def produce(t, carry):
         k, h = lax.rem(t, 4), lax.div(t, 4)
@@ -592,10 +595,8 @@
             fourth_wait(col)
             mult[col] = dot(wraw[:, :, col].reshape(mult.shape[1:]), dense[...], 1, 0)
 
-        @pl.when(t == 4)
-        def _():
-            for h, way in raw_halves[1]:
-                pl.when(comes[way])(lambda way=way, h=h: raw_copy(way, h).wait_recv())
+        for now in range(split):
+            pl.when(t == 4 * now)(lambda now=now: raw_wait(now))
 
         @pl.when(active)
         def _():
@@ -717,7 +718,7 @@
     mine, n = diag_block.shape
     rows, width = panel.shape
     columns = trailing.shape[1]
-    split = 2
+    split = 3
     planes = n_r // 2 * n_d
     piece = columns // (2 * planes)
     parts = []
@@ -731,7 +732,7 @@
     vmem, anywhere = pl.BlockSpec(memory_space=pltpu.VMEM), pl.BlockSpec(memory_space=pl.ANY)
     dma = pltpu.SemaphoreType.DMA
     sems = [
-        dma, dma, dma, dma((n_c,)), dma, dma((planes,)), dma, dma, dma, dma((3, 3)), dma((3, 3)),
+        dma, dma, dma, dma((n_c,)), dma, dma((planes,)), dma, dma, dma, dma((3, 4)), dma((3, 4)),
         dma((len(parts),)), dma((len(parts),)), dma((n_c,)), dma, dma((planes, n_c)), dma((planes, n_c)), dma((n_c,)), dma((n_c,)),
         dma((4, split)), dma((4, split)),
     ]
@@ -761,7 +762,7 @@
 
 def body(sizes, diag_block, panel_rows, trailing):
     n_r, n_c, n_d = sizes
-    if sizes == (4, 4, 2) and panel_rows.shape[0] % 16 == 0:
+    if sizes == (4, 4, 2) and panel_rows.shape[0] % 48 == 0:
         return place_call(*near_call(sizes, diag_block, panel_rows, trailing))
     position = (lax.axis_index("row") * n_c + lax.axis_index("col")) * n_d + lax.axis_index("depth")
     mine = diag_block.shape[0]

time: 113 us -> 109 us (0.965); the launches traced: 113 us -> 107 us
  Pallas kernels: 112 us -> 106 us
    pallas_call x1, Pallas kernels: 110 us -> 103 us  [near_call(): pl.pallas_call(functools.partial(near, sizes, parts, split), out_shape=(j...]
where the time goes in v5:
time: 109 us; the launch traced here: 107 us
  Pallas kernels  106 us (97%)
    pallas_call x1, Pallas kernels, near_call(): pl.pallas_call(functools.partial(near, sizes, parts, split), out_shape=(j...  103 us
    pallas_call x1, Pallas kernels, place_call(): pl.pallas_call(place, out_shape=tuple((jax.ShapeDtypeStruct(x.shape, x.dt...  2.69 us

profile of v5, /device:TPU:11, one launch (start us, length us, event | category | flops | bytes accessed | tf_op | source)
XLA Modules:
  0.0 106.6 jit_solution(5340068303112992118)
XLA Ops:
  0.6 103.2 %shard_map.58 = (f32[16,512]{1,0:T(8,128)S(1)}, f32[1008,512]{1,0:T(8,128)S(1)}, f32[4032,256]{1,0:T(8,128)S(1)}) custom-call(f32[16,512]{1,0:T(8,128)} %diag_ref.1, f32[1008,512]{1,0:T(8,128)} %panel.1, f32[4032,256]{1,0:T(8,128)} %trailing.1), custom_call_target="tpu_custom_call" | custom-call | tf_op jit(solution)/shard_map/pallas_call | solution.py:740
  103.9 2.7 %shard_map.59 = (f32[16,512]{1,0:T(8,128)}, f32[1008,512]{1,0:T(8,128)}, f32[4032,256]{1,0:T(8,128)}) custom-call(f32[16,512]{1,0:T(8,128)S(1)} %get-tuple-element.6.own, f32[1008,512]{1,0:T(8,128)S(1)} %get-tuple-element.7.solved, f32[4032,256]{1,0:T(8,128)S(1)} %get-tuple-element.8.updated), custom_call_target="tpu_custom_call" | custom-call | tf_op jit(solution)/shard_map/pallas_call | solution.py:706
